TPU v7x, 32 devices: a whole 2x2x4 slice. The times are simulated.
32 devices in a mesh: row: 8 (over z, y), col: 4 (over x, core).
Axes of the slice: x: 2, y: 2, z: 4, core: 2. Of those that a mesh axis runs over, the one named last changes fastest.
Arguments:
- matrix: float32 [4096, 4096], P('row', 'col'), may hold values from -0.92 to 1.92, as said below
Outputs:
- inverse: float32 [4096, 4096], P('row', 'col')
- residual_norms: float32 [4], replicated
Inputs may be any that keep to these rules, and one draw needn't show every extreme that they name: matrix is exactly symmetric and positive definite; all its eigenvalues lie between 0.08 and 1.92.
All inputs are finite; a program needn't handle non-finite values.
Results may differ from a plain program's by a relative error of at most 0.0017.
The roundings to bfloat16 on the way count: a program that leaves them out, or rounds other values in their place, can miss the bound.
Values may be sent and summed in bfloat16 or wider, within the bound.
A program may use at most 64 MiB of HBM per device.

v0:
```python
import jax
import jax.numpy as jnp
from jax import lax
from jax.sharding import PartitionSpec as P

N = 4096
ITERS = 4


def shards(matrix):
    row_count, col_count = matrix.shape
    row_index = lax.axis_index("row")
    col_index = lax.axis_index("col")
    sq_total = lax.psum(jnp.sum(matrix * matrix), ("row", "col"))
    start_scale = jnp.sqrt(jnp.float32(N)) / jnp.sqrt(sq_total)
    global_rows = row_index * row_count + lax.broadcasted_iota(jnp.int32, (row_count, col_count), 0)
    global_cols = col_index * col_count + lax.broadcasted_iota(jnp.int32, (row_count, col_count), 1)
    eye_block = (global_rows == global_cols).astype(jnp.float32)
    mat_low = matrix.astype(jnp.bfloat16)
    panel_rows = lax.all_gather(mat_low, "col", axis=1, tiled=True)
    current = start_scale * eye_block
    partial_list = []
    for iteration in range(ITERS):
        cur_low = current.astype(jnp.bfloat16)
        product = jnp.dot(
            panel_rows,
            lax.all_gather(cur_low, "row", axis=0, tiled=True),
            preferred_element_type=jnp.float32,
        )
        residual = eye_block - product
        local_sum = jnp.sum(residual * residual)
        partial_list.append(local_sum)
        shift_low = (eye_block + residual).astype(jnp.bfloat16)
        iterate_rows = lax.all_gather(cur_low, "col", axis=1, tiled=True)
        current = jnp.dot(
            iterate_rows,
            lax.all_gather(shift_low, "row", axis=0, tiled=True),
            preferred_element_type=jnp.float32,
        )
    summed = lax.psum(jnp.stack(partial_list), ("row", "col"))
    residual_norms = jnp.sqrt(summed / N)
    return (current, residual_norms)


def solution(mesh):
    in_specs = (P("row", "col"),)
    out_specs = (P("row", "col"), P())
    return jax.shard_map(shards, mesh=mesh, in_specs=in_specs, out_specs=out_specs, check_vma=False)
```

profile of v0, /device:TPU:0, one launch (start us, length us, event | category | flops | bytes accessed | tf_op | source)
XLA Modules:
  0.0 1244.2 jit_solution(14768718448786911574)
XLA Ops:
  7.2 4.3 fusion.5
  11.6 42.5 %psum.14 = f32[]{:T(128)} all-reduce(f32[]{:T(128)} %get-tuple-element.8), channel_id=1, replica_groups=mesh['row'=8,'col'=4] {'row','col'}, use_global_device_ids=true, to_apply=%region_1.0 | all-reduce | flops 1 | bytes 8 | tf_op jit(solution)/shard_map/psum | solution.py:14
  54.8 1.2 fusion
  56.1 0.7 all-gather.14.cloned.1.call-update
  56.9 124.6 %all-gather.16.cloned.1.call-done = bf16[4096,1024]{0,1:T(8,128)(2,1)} async-done(((bf16[512,1024]{0,1:T(8,128)(2,1)}), bf16[4096,1024]{0,1:T(8,128)(2,1)}) %all-gather.16.cloned.1.call-update) | async-done | bytes 8388624 | tf_op jit(solution)/shard_map/all_gather | solution.py:27
  181.5 10.1 fusion.1
  191.7 24.1 %all-gather.14.cloned.1.call-done = bf16[512,4096]{0,1:T(8,128)(2,1)} async-done(((bf16[512,1024]{0,1:T(8,128)(2,1)}), bf16[512,4096]{0,1:T(8,128)(2,1)}) %all-gather.14.cloned.1.call-update) | async-done | bytes 4194320 | tf_op jit(solution)/shard_map/all_gather | solution.py:34
  215.7 127.4 %all-gather.20.cloned.1.call-done = bf16[4096,1024]{0,1:T(8,128)(2,1)} async-done(((bf16[512,1024]{0,1:T(8,128)(2,1)}), bf16[4096,1024]{0,1:T(8,128)(2,1)}) %all-gather.20.cloned.1.call-update) | async-done | bytes 8388624 | tf_op jit(solution)/shard_map/all_gather | solution.py:37
  343.2 10.2 convolution_convert_fusion.2
  353.4 0.5 all-gather.22.cloned.1.call-update
  354.0 0.5 all-gather.26.cloned.1.call-start
  354.5 121.7 %all-gather.24.cloned.1.call-done = bf16[4096,1024]{1,0:T(8,128)(2,1)} async-done(((bf16[512,1024]{1,0:T(8,128)(2,1)}), bf16[4096,1024]{1,0:T(8,128)(2,1)}) %all-gather.24.cloned.1.call-update) | async-done | bytes 8388624 | tf_op jit(solution)/shard_map/all_gather | solution.py:27
  476.2 10.9 fusion.2
  487.1 23.1 %all-gather.22.cloned.1.call-done = bf16[512,4096]{1,0:T(8,128)(2,1)} async-done(((bf16[512,1024]{1,0:T(8,128)(2,1)}), bf16[512,4096]{1,0:T(8,128)(2,1)}) %all-gather.22.cloned.1.call-update) | async-done | bytes 4194320 | tf_op jit(solution)/shard_map/all_gather | solution.py:34
  510.3 127.0 %all-gather.26.cloned.1.call-done = bf16[4096,1024]{0,1:T(8,128)(2,1)} async-done(((bf16[512,1024]{0,1:T(8,128)(2,1)}), bf16[4096,1024]{0,1:T(8,128)(2,1)}) %all-gather.26.cloned.1.call-update) | async-done | bytes 8388624 | tf_op jit(solution)/shard_map/all_gather | solution.py:37
  637.3 10.2 convolution_convert_fusion.1
  647.5 0.7 all-gather.28.cloned.1.call-update
  648.2 0.2 all-gather.32.cloned.1.call-start
  648.4 121.9 %all-gather.30.cloned.1.call-done = bf16[4096,1024]{1,0:T(8,128)(2,1)} async-done(((bf16[512,1024]{1,0:T(8,128)(2,1)}), bf16[4096,1024]{1,0:T(8,128)(2,1)}) %all-gather.30.cloned.1.call-update) | async-done | bytes 8388624 | tf_op jit(solution)/shard_map/all_gather | solution.py:27
  770.3 10.9 fusion.3
  781.2 23.3 %all-gather.28.cloned.1.call-done = bf16[512,4096]{1,0:T(8,128)(2,1)} async-done(((bf16[512,1024]{1,0:T(8,128)(2,1)}), bf16[512,4096]{1,0:T(8,128)(2,1)}) %all-gather.28.cloned.1.call-update) | async-done | bytes 4194320 | tf_op jit(solution)/shard_map/all_gather | solution.py:34
  804.5 126.9 %all-gather.32.cloned.1.call-done = bf16[4096,1024]{0,1:T(8,128)(2,1)} async-done(((bf16[512,1024]{0,1:T(8,128)(2,1)}), bf16[4096,1024]{0,1:T(8,128)(2,1)}) %all-gather.32.cloned.1.call-update) | async-done | bytes 8388624 | tf_op jit(solution)/shard_map/all_gather | solution.py:37
  931.4 10.2 convolution_convert_fusion
  941.6 0.5 all-gather.34.cloned.1.call-update
  942.2 0.3 all-gather.38.cloned.1.call-start
  942.4 122.0 %all-gather.36.cloned.1.call-done = bf16[4096,1024]{1,0:T(8,128)(2,1)} async-done(((bf16[512,1024]{1,0:T(8,128)(2,1)}), bf16[4096,1024]{1,0:T(8,128)(2,1)}) %all-gather.36.cloned.1.call-update) | async-done | bytes 8388624 | tf_op jit(solution)/shard_map/all_gather | solution.py:27
  1064.4 12.9 %multiply_reduce_fusion.3 = (f32[]{:T(128)}, f32[]{:T(128)}, f32[]{:T(128)}, f32[]{:T(128)}, bf16[512,1024]{0,1:T(8,128)(2,1)}) fusion(f32[1024,512]{1,0:T(8,128)S(1)} %get-tuple-element.10, s32[512]{0:T(512)S(1)} %iota_add_fusion.1, s32[1024]{0:T(1024)S(1)} %iota_add_fusion, f32[1024,512]{1,0:T(8,128)} %get-tuple-element.12, ...), kind=kOutput, calls=%fused_computation.17 | convolution fusion | flops 4303355904 | bytes 19929104 | tf_op jit(solution)/shard_map/dot_general | solution.py:25
  1077.4 2.6 pad_maximum_fusion
  1079.9 39.1 %psum.15 = f32[4]{0:T(128)S(1)} all-reduce(f32[4]{0:T(128)S(1)} %pad_maximum_fusion), channel_id=1, replica_groups=mesh['row'=8,'col'=4] {'row','col'}, use_global_device_ids=true, to_apply=%region_6.0 | all-reduce | flops 4 | bytes 32 | tf_op jit(solution)/shard_map/psum | solution.py:40
  1119.1 0.5 multiply_sqrt_fusion
  1119.6 107.3 %all-gather.38.cloned.1.call-done = bf16[4096,1024]{0,1:T(8,128)(2,1)} async-done(((bf16[512,1024]{0,1:T(8,128)(2,1)}), bf16[4096,1024]{0,1:T(8,128)(2,1)}) %all-gather.38.cloned.1.call-update) | async-done | bytes 8388624 | tf_op jit(solution)/shard_map/all_gather | solution.py:37
  1226.9 10.5 fusion.6
  (23 shorter events, 0.6 us)
Async XLA Ops:
  7.2 49.7 %all-gather.18.cloned.1.call-start = ((), (), s32[]{:S(2)}) async-start(), calls=%async_computation.2 | async-start | bytes 5242880 | tf_op jit(solution)/shard_map/all_gather | solution.py:20
  11.5 170.0 %all-gather.16.cloned.1.call-start = ((), (), s32[]{:S(2)}) async-start(), calls=%async_computation.1 | async-start | bytes 9437184 | tf_op jit(solution)/shard_map/all_gather | solution.py:27
  56.1 159.7 %all-gather.14.cloned.1.call-start = ((), (), s32[]{:S(2)}) async-start(), calls=%async_computation | async-start | bytes 5242880 | tf_op jit(solution)/shard_map/all_gather | solution.py:34
  56.8 286.4 %all-gather.20.cloned.1.call-start = ((), (), s32[]{:S(2)}) async-start(), calls=%async_computation.3 | async-start | bytes 9437184 | tf_op jit(solution)/shard_map/all_gather | solution.py:37
  191.6 284.6 %all-gather.24.cloned.1.call-start = ((), (), s32[]{:S(2)}) async-start(), calls=%async_computation.5 | async-start | bytes 9437184 | tf_op jit(solution)/shard_map/all_gather | solution.py:27
  353.4 156.9 %all-gather.22.cloned.1.call-start = ((), (), s32[]{:S(2)}) async-start(), calls=%async_computation.4 | async-start | bytes 5242880 | tf_op jit(solution)/shard_map/all_gather | solution.py:34
  354.0 283.3 %all-gather.26.cloned.1.call-start = ((), (), s32[]{:S(2)}) async-start(), calls=%async_computation.6 | async-start | bytes 9437184 | tf_op jit(solution)/shard_map/all_gather | solution.py:37
  487.1 283.2 %all-gather.30.cloned.1.call-start = ((), (), s32[]{:S(2)}) async-start(), calls=%async_computation.8 | async-start | bytes 9437184 | tf_op jit(solution)/shard_map/all_gather | solution.py:27
  647.5 157.0 %all-gather.28.cloned.1.call-start = ((), (), s32[]{:S(2)}) async-start(), calls=%async_computation.7 | async-start | bytes 5242880 | tf_op jit(solution)/shard_map/all_gather | solution.py:34
  648.2 283.2 %all-gather.32.cloned.1.call-start = ((), (), s32[]{:S(2)}) async-start(), calls=%async_computation.9 | async-start | bytes 9437184 | tf_op jit(solution)/shard_map/all_gather | solution.py:37
  781.2 283.2 %all-gather.36.cloned.1.call-start = ((), (), s32[]{:S(2)}) async-start(), calls=%async_computation.11 | async-start | bytes 9437184 | tf_op jit(solution)/shard_map/all_gather | solution.py:27
  941.6 178.0 %all-gather.34.cloned.1.call-start = ((), (), s32[]{:S(2)}) async-start(), calls=%async_computation.10 | async-start | bytes 5242880 | tf_op jit(solution)/shard_map/all_gather | solution.py:34
  942.2 284.7 %all-gather.38.cloned.1.call-start = ((), (), s32[]{:S(2)}) async-start(), calls=%async_computation.12 | async-start | bytes 9437184 | tf_op jit(solution)/shard_map/all_gather | solution.py:37
Sparse Core Ops, SparseCore 0:
  11.6 37.4 all-gather.17
  56.2 125.2 all-gather.15
  183.1 32.6 all-gather.13
  218.2 124.9 all-gather.19
  353.5 122.6 all-gather.23
  477.6 32.6 all-gather.21
  512.3 124.9 all-gather.25
  647.6 122.6 all-gather.29
  771.9 32.6 all-gather.27
  806.4 124.9 all-gather.31
  941.7 122.6 all-gather.35
  1065.8 33.3 all-gather.33
  1101.2 125.6 all-gather.37
where the time goes:
time: 1250 us; the launch traced here: 1240 us
  waiting for transfers between devices  1050 us (84%)
  matrix products  85.8 us (7%)
  blocking collectives  81.7 us (7%)
  between operations  14.9 us (1%)
    all_gather x4, waiting for transfers between devices, shards(): lax.all_gather(cur_low, 'row', axis=0, tiled=True)  490 us
    all_gather x4, waiting for transfers between devices, shards(): lax.all_gather(shift_low, 'row', axis=0, tiled=True)  489 us
    all_gather x4, waiting for transfers between devices, shards(): iterate_rows = lax.all_gather(cur_low, 'col', axis=1, tiled=True)  70.5 us
    dot_general x4, matrix products, shards(): jnp.dot(panel_rows, lax.all_gather(cur_low, 'row', axis=0, tiled=True), p...  44.8 us
    psum x1, blocking collectives, shards(): sq_total = lax.psum(jnp.sum(matrix * matrix), ('row', 'col'))  42.5 us
    dot_general x4, matrix products, shards(): jnp.dot(iterate_rows, lax.all_gather(shift_low, 'row', axis=0, tiled=True...  41 us
    psum x1, blocking collectives, shards(): summed = lax.psum(jnp.stack(partial_list), ('row', 'col'))  39.1 us
  transfers between devices with their start and end apart: 13, of which 11 were waited for; matrix products, arithmetic and copies ran while one was open for 4% of the time, Pallas kernels for 0%

commit v1 on v0

--- a/solution.py
+++ b/solution.py
@@ -1,3 +1,4 @@
+import functools
 import jax
 import jax.numpy as jnp
 from jax import lax
@@ -5,6 +6,22 @@
 
 N = 4096
 ITERS = 4
+
+
+def fix_inputs_on_mesh(frame, named_axis):
+    n_lanes = jax.lax.axis_size(named_axis)
+    earlier = sorted(((dd, (dd + 1) % n_lanes) for dd in range(n_lanes)))
+    out_arr = frame
+    crops = [out_arr]
+    for jj in range(1, n_lanes):
+        out_arr = jax.lax.ppermute(out_arr, axis_name=named_axis, perm=earlier)
+        crops.insert(0, out_arr)
+    outcome_arr = jnp.concatenate(crops, axis=1)
+    b_now = jax.lax.axis_index(named_axis) + 1
+    return jnp.roll(outcome_arr, b_now * frame.shape[1], axis=1)
+
+
+map_set = functools.partial(fix_inputs_on_mesh, named_axis="col")
 
 
 def shards(matrix):
@@ -31,7 +48,7 @@
         local_sum = jnp.sum(residual * residual)
         partial_list.append(local_sum)
         shift_low = (eye_block + residual).astype(jnp.bfloat16)
-        iterate_rows = lax.all_gather(cur_low, "col", axis=1, tiled=True)
+        iterate_rows = map_set(cur_low)
         current = jnp.dot(
             iterate_rows,
             lax.all_gather(shift_low, "row", axis=0, tiled=True),

time: 1250 us -> 1170 us (0.936)
  waiting for transfers between devices: 1050 us -> 926 us
  matrix products: 85.8 us -> 110 us
  blocking collectives: 81.7 us -> 99 us
    all_gather x4, waiting for transfers between devices: 489 us -> 276 us  [shards(): lax.all_gather(shift_low, 'row', axis=0, tiled=True)]
    ppermute x0 -> x12, waiting for transfers between devices: none -> 157 us  [fix_inputs_on_mesh(): out_arr = jax.lax.ppermute(out_arr, axis_name=named_axis, perm=earlier)]
    all_gather x4 -> x0, waiting for transfers between devices: 70.5 us -> none  [shards(): iterate_rows = lax.all_gather(cur_low, 'col', axis=1, tiled=True)]
    dot_general x4, matrix products: 41 us -> 64 us  [shards(): jnp.dot(iterate_rows, lax.all_gather(shift_low, 'row', axis=0, tiled=True...]
    psum x1, blocking collectives: 39.1 us -> 56.5 us  [shards(): summed = lax.psum(jnp.stack(partial_list), ('row', 'col'))]
  transfers between devices with their start and end apart: 13 -> 21, of which waited for: 11 -> 19; matrix products, arithmetic and copies ran while one was open for 4% -> 0% of each run, Pallas kernels for 0% -> 0%
where the time goes in v1:
time: 1170 us; the launch traced here: 1160 us
  waiting for transfers between devices  926 us (79%)
  matrix products  110 us (9%)
  blocking collectives  99 us (8%)
  between operations  15.3 us (1%)
    all_gather x4, waiting for transfers between devices, shards(): lax.all_gather(cur_low, 'row', axis=0, tiled=True)  493 us
    all_gather x4, waiting for transfers between devices, shards(): lax.all_gather(shift_low, 'row', axis=0, tiled=True)  276 us
    ppermute x12, waiting for transfers between devices, fix_inputs_on_mesh(): out_arr = jax.lax.ppermute(out_arr, axis_name=named_axis, perm=earlier)  157 us
    dot_general x4, matrix products, shards(): jnp.dot(iterate_rows, lax.all_gather(shift_low, 'row', axis=0, tiled=True...  64 us
    psum x1, blocking collectives, shards(): summed = lax.psum(jnp.stack(partial_list), ('row', 'col'))  56.5 us
    dot_general x4, matrix products, shards(): jnp.dot(panel_rows, lax.all_gather(cur_low, 'row', axis=0, tiled=True), p...  45.9 us
    psum x1, blocking collectives, shards(): sq_total = lax.psum(jnp.sum(matrix * matrix), ('row', 'col'))  42.5 us
  transfers between devices with their start and end apart: 21, of which 19 were waited for; matrix products, arithmetic and copies ran while one was open for 0% of the time, Pallas kernels for 0%

profile of v1, /device:TPU:0, one launch (start us, length us, event | category | flops | bytes accessed | tf_op | source)
XLA Modules:
  0.0 1160.9 jit_solution(14153085332242222172)
XLA Ops:
  7.2 4.3 fusion.62
  11.6 42.5 %psum.14 = f32[]{:T(128)} all-reduce(f32[]{:T(128)} %get-tuple-element.9), channel_id=1, replica_groups=mesh['row'=8,'col'=4] {'row','col'}, use_global_device_ids=true, to_apply=%region_1.0 | all-reduce | flops 1 | bytes 8 | tf_op jit(solution)/shard_map/psum | solution.py:31
  54.8 1.3 fusion.40
  56.2 125.3 %all-gather.10.cloned.1.call-done = bf16[4096,1024]{0,1:T(8,128)(2,1)} async-done(((bf16[512,1024]{0,1:T(8,128)(2,1)}), bf16[4096,1024]{0,1:T(8,128)(2,1)}) %all-gather.10.cloned.1.call-update) | async-done | bytes 8388624 | tf_op jit(solution)/shard_map/all_gather | solution.py:44
  181.5 10.8 fusion.41
  192.4 14.2 %collective-permute-done = bf16[512,1024]{0,1:T(8,128)(2,1)S(1)} collective-permute-done((bf16[512,1024]{0,1:T(8,128)(2,1)S(1)}, bf16[512,1024]{0,1:T(8,128)(2,1)S(1)}, u32[]{:S(2)}, u32[]{:S(2)}) %collective-permute-start) | collective-permute-done | bytes 1048608 | tf_op jit(solution)/shard_map/ppermute | solution.py:17
  206.6 14.2 %collective-permute-done.1 = bf16[512,1024]{0,1:T(8,128)(2,1)S(1)} collective-permute-done((bf16[512,1024]{0,1:T(8,128)(2,1)S(1)}, bf16[512,1024]{0,1:T(8,128)(2,1)S(1)}, u32[]{:S(2)}, u32[]{:S(2)}) %collective-permute-start.1) | collective-permute-done | bytes 1048608 | tf_op jit(solution)/shard_map/ppermute | solution.py:17
  221.1 14.3 %collective-permute-done.2 = bf16[512,1024]{0,1:T(8,128)(2,1)} collective-permute-done((bf16[512,1024]{0,1:T(8,128)(2,1)S(1)}, bf16[512,1024]{0,1:T(8,128)(2,1)}, u32[]{:S(2)}, u32[]{:S(2)}) %collective-permute-start.2) | collective-permute-done | bytes 1048608 | tf_op jit(solution)/shard_map/ppermute | solution.py:17
  235.4 80.2 %all-gather.14.cloned.1.call-done = bf16[4096,1024]{0,1:T(8,128)(2,1)} async-done(((bf16[512,1024]{0,1:T(8,128)(2,1)}), bf16[4096,1024]{0,1:T(8,128)(2,1)}) %all-gather.14.cloned.1.call-update) | async-done | bytes 8388624 | tf_op jit(solution)/shard_map/all_gather | solution.py:54
  315.6 24.7 %fusion.45 = bf16[512,1024]{1,0:T(8,128)(2,1)} fusion(bf16[4096,1024]{0,1:T(8,128)(2,1)} %all-gather.14.cloned.1.call-done, s32[]{:T(128)S(6)} %select_n.17, bf16[512,1024]{0,1:T(8,128)(2,1)} %collective-permute-done.2, bf16[512,1024]{0,1:T(8,128)(2,1)S(1)} %collective-permute-done.1, bf16[512,1024]{0,1:T(8,128)(2,1)S(1)} %collective-permute-done, ...), kind=kOutput, calls=%fused_computation.83 | convolution fusion | flops 4329046016 | bytes 13631492 | tf_op jit(solution)/shard_map/dot_general | solution.py:52
  340.4 122.8 %all-gather.16.cloned.1.call-done = bf16[4096,1024]{1,0:T(8,128)(2,1)} async-done(((bf16[512,1024]{1,0:T(8,128)(2,1)}), bf16[4096,1024]{1,0:T(8,128)(2,1)}) %all-gather.16.cloned.1.call-update) | async-done | bytes 8388624 | tf_op jit(solution)/shard_map/all_gather | solution.py:44
  463.1 10.9 fusion.42
  474.2 14.2 %collective-permute-done.3 = bf16[512,1024]{1,0:T(8,128)(2,1)S(1)} collective-permute-done((bf16[512,1024]{1,0:T(8,128)(2,1)S(1)}, bf16[512,1024]{1,0:T(8,128)(2,1)S(1)}, u32[]{:S(2)}, u32[]{:S(2)}) %collective-permute-start.3) | collective-permute-done | bytes 1048608 | tf_op jit(solution)/shard_map/ppermute | solution.py:17
  488.4 14.2 %collective-permute-done.4 = bf16[512,1024]{1,0:T(8,128)(2,1)S(1)} collective-permute-done((bf16[512,1024]{1,0:T(8,128)(2,1)S(1)}, bf16[512,1024]{1,0:T(8,128)(2,1)S(1)}, u32[]{:S(2)}, u32[]{:S(2)}) %collective-permute-start.4) | collective-permute-done | bytes 1048608 | tf_op jit(solution)/shard_map/ppermute | solution.py:17
  502.8 14.3 %collective-permute-done.5 = bf16[512,1024]{1,0:T(8,128)(2,1)} collective-permute-done((bf16[512,1024]{1,0:T(8,128)(2,1)S(1)}, bf16[512,1024]{1,0:T(8,128)(2,1)}, u32[]{:S(2)}, u32[]{:S(2)}) %collective-permute-start.5) | collective-permute-done | bytes 1048608 | tf_op jit(solution)/shard_map/ppermute | solution.py:17
  517.1 80.2 %all-gather.18.cloned.1.call-done = bf16[4096,1024]{0,1:T(8,128)(2,1)} async-done(((bf16[512,1024]{0,1:T(8,128)(2,1)}), bf16[4096,1024]{0,1:T(8,128)(2,1)}) %all-gather.18.cloned.1.call-update) | async-done | bytes 8388624 | tf_op jit(solution)/shard_map/all_gather | solution.py:54
  597.3 13.0 %fusion.48 = bf16[512,1024]{1,0:T(8,128)(2,1)} fusion(bf16[4096,1024]{0,1:T(8,128)(2,1)} %all-gather.18.cloned.1.call-done, s32[]{:T(128)S(6)} %select_n.17, bf16[512,1024]{1,0:T(8,128)(2,1)} %collective-permute-done.5, bf16[512,1024]{1,0:T(8,128)(2,1)S(1)} %collective-permute-done.4, bf16[512,1024]{1,0:T(8,128)(2,1)S(1)} %collective-permute-done.3, ...), kind=kOutput, calls=%fused_computation.84 | convolution fusion | flops 4329046016 | bytes 13631492 | tf_op jit(solution)/shard_map/dot_general | solution.py:52
  610.6 122.5 %all-gather.20.cloned.1.call-done = bf16[4096,1024]{1,0:T(8,128)(2,1)} async-done(((bf16[512,1024]{1,0:T(8,128)(2,1)}), bf16[4096,1024]{1,0:T(8,128)(2,1)}) %all-gather.20.cloned.1.call-update) | async-done | bytes 8388624 | tf_op jit(solution)/shard_map/all_gather | solution.py:44
  733.1 10.9 fusion.43
  744.2 14.2 %collective-permute-done.6 = bf16[512,1024]{1,0:T(8,128)(2,1)S(1)} collective-permute-done((bf16[512,1024]{1,0:T(8,128)(2,1)S(1)}, bf16[512,1024]{1,0:T(8,128)(2,1)S(1)}, u32[]{:S(2)}, u32[]{:S(2)}) %collective-permute-start.6) | collective-permute-done | bytes 1048608 | tf_op jit(solution)/shard_map/ppermute | solution.py:17
  758.4 14.2 %collective-permute-done.7 = bf16[512,1024]{1,0:T(8,128)(2,1)S(1)} collective-permute-done((bf16[512,1024]{1,0:T(8,128)(2,1)S(1)}, bf16[512,1024]{1,0:T(8,128)(2,1)S(1)}, u32[]{:S(2)}, u32[]{:S(2)}) %collective-permute-start.7) | collective-permute-done | bytes 1048608 | tf_op jit(solution)/shard_map/ppermute | solution.py:17
  772.8 14.3 %collective-permute-done.8 = bf16[512,1024]{1,0:T(8,128)(2,1)} collective-permute-done((bf16[512,1024]{1,0:T(8,128)(2,1)S(1)}, bf16[512,1024]{1,0:T(8,128)(2,1)}, u32[]{:S(2)}, u32[]{:S(2)}) %collective-permute-start.8) | collective-permute-done | bytes 1048608 | tf_op jit(solution)/shard_map/ppermute | solution.py:17
  787.1 80.2 %all-gather.22.cloned.1.call-done = bf16[4096,1024]{0,1:T(8,128)(2,1)} async-done(((bf16[512,1024]{0,1:T(8,128)(2,1)}), bf16[4096,1024]{0,1:T(8,128)(2,1)}) %all-gather.22.cloned.1.call-update) | async-done | bytes 8388624 | tf_op jit(solution)/shard_map/all_gather | solution.py:54
  867.3 13.0 %fusion.51 = bf16[512,1024]{1,0:T(8,128)(2,1)} fusion(bf16[4096,1024]{0,1:T(8,128)(2,1)} %all-gather.22.cloned.1.call-done, s32[]{:T(128)S(6)} %select_n.17, bf16[512,1024]{1,0:T(8,128)(2,1)} %collective-permute-done.8, bf16[512,1024]{1,0:T(8,128)(2,1)S(1)} %collective-permute-done.7, bf16[512,1024]{1,0:T(8,128)(2,1)S(1)} %collective-permute-done.6, ...), kind=kOutput, calls=%fused_computation.85 | convolution fusion | flops 4329046016 | bytes 13631492 | tf_op jit(solution)/shard_map/dot_general | solution.py:52
  880.6 122.5 %all-gather.24.cloned.1.call-done = bf16[4096,1024]{1,0:T(8,128)(2,1)} async-done(((bf16[512,1024]{1,0:T(8,128)(2,1)}), bf16[4096,1024]{1,0:T(8,128)(2,1)}) %all-gather.24.cloned.1.call-update) | async-done | bytes 8388624 | tf_op jit(solution)/shard_map/all_gather | solution.py:44
  1003.1 13.4 %multiply_reduce_fusion.3 = (f32[]{:T(128)}, f32[]{:T(128)}, f32[]{:T(128)}, f32[]{:T(128)}, bf16[512,1024]{0,1:T(8,128)(2,1)}) fusion(f32[1024,512]{1,0:T(8,128)} %get-tuple-element.11, s32[512]{0:T(512)S(1)} %iota_add_fusion.1, s32[1024]{0:T(1024)S(1)} %iota_add_fusion, f32[1024,512]{1,0:T(8,128)} %get-tuple-element.13, ...), kind=kOutput, calls=%fused_computation.81 | convolution fusion | flops 4303355904 | bytes 19929104 | tf_op jit(solution)/shard_map/dot_general | solution.py:42
  1016.6 14.2 %collective-permute-done.9 = bf16[512,1024]{1,0:T(8,128)(2,1)S(1)} collective-permute-done((bf16[512,1024]{1,0:T(8,128)(2,1)S(1)}, bf16[512,1024]{1,0:T(8,128)(2,1)S(1)}, u32[]{:S(2)}, u32[]{:S(2)}) %collective-permute-start.9) | collective-permute-done | bytes 1048608 | tf_op jit(solution)/shard_map/ppermute | solution.py:17
  1030.8 14.2 %collective-permute-done.10 = bf16[512,1024]{1,0:T(8,128)(2,1)S(1)} collective-permute-done((bf16[512,1024]{1,0:T(8,128)(2,1)S(1)}, bf16[512,1024]{1,0:T(8,128)(2,1)S(1)}, u32[]{:S(2)}, u32[]{:S(2)}) %collective-permute-start.10) | collective-permute-done | bytes 1048608 | tf_op jit(solution)/shard_map/ppermute | solution.py:17
  1045.0 2.6 pad_maximum_fusion
  1047.7 56.5 %psum.15 = f32[4]{0:T(128)S(1)} all-reduce(f32[4]{0:T(128)S(1)} %pad_maximum_fusion), channel_id=1, replica_groups=mesh['row'=8,'col'=4] {'row','col'}, use_global_device_ids=true, to_apply=%region_6.8 | all-reduce | flops 4 | bytes 32 | tf_op jit(solution)/shard_map/psum | solution.py:57
  1104.7 35.8 %all-gather.26.cloned.1.call-done = bf16[4096,1024]{0,1:T(8,128)(2,1)} async-done(((bf16[512,1024]{0,1:T(8,128)(2,1)}), bf16[4096,1024]{0,1:T(8,128)(2,1)}) %all-gather.26.cloned.1.call-update) | async-done | bytes 8388624 | tf_op jit(solution)/shard_map/all_gather | solution.py:54
  1140.5 13.3 %fusion.4 = f32[512,1024]{1,0:T(8,128)} fusion(bf16[4096,1024]{0,1:T(8,128)(2,1)} %all-gather.26.cloned.1.call-done, s32[]{:T(128)S(6)} %select_n.17, bf16[512,1024]{1,0:T(8,128)(2,1)} %collective-permute-done.11, bf16[512,1024]{1,0:T(8,128)(2,1)S(1)} %collective-permute-done.10, bf16[512,1024]{1,0:T(8,128)(2,1)S(1)} %collective-permute-done.9, ...), kind=kOutput, calls=%fused_computation.45 | convolution fusion | flops 4328521728 | bytes 14680068 | tf_op jit(solution)/shard_map/dot_general | solution.py:52
  (43 shorter events, 2.4 us)
Async XLA Ops:
  7.2 49.0 %all-gather.12.cloned.1.call-start = ((), (), s32[]{:S(2)}) async-start(), calls=%async_computation.1 | async-start | bytes 5242880 | tf_op jit(solution)/shard_map/all_gather | solution.py:37
  11.5 170.0 %all-gather.10.cloned.1.call-start = ((), (), s32[]{:S(2)}) async-start(), calls=%async_computation | async-start | bytes 9437184 | tf_op jit(solution)/shard_map/all_gather | solution.py:44
  56.1 136.2 %copy-start = (bf16[512,1024]{0,1:T(8,128)(2,1)S(1)}, bf16[512,1024]{0,1:T(8,128)(2,1)}, u32[]{:S(2)}) copy-start(bf16[512,1024]{0,1:T(8,128)(2,1)} %fusion.40) | copy-start | bytes 3145732
  56.1 259.4 %all-gather.14.cloned.1.call-start = ((), (), s32[]{:S(2)}) async-start(), calls=%async_computation.2 | async-start | bytes 9437184 | tf_op jit(solution)/shard_map/all_gather | solution.py:54
  192.3 270.9 %all-gather.16.cloned.1.call-start = ((), (), s32[]{:S(2)}) async-start(), calls=%async_computation.3 | async-start | bytes 9437184 | tf_op jit(solution)/shard_map/all_gather | solution.py:44
  192.3 14.3 %collective-permute-start = (bf16[512,1024]{0,1:T(8,128)(2,1)S(1)}, bf16[512,1024]{0,1:T(8,128)(2,1)S(1)}, u32[]{:S(2)}, u32[]{:S(2)}) collective-permute-start(bf16[512,1024]{0,1:T(8,128)(2,1)S(1)} %copy-done), channel_id=1, source_target_pairs={{0,1},{1,2},{2,3},{3,0},{4,5},{5,6},{6,7},{7,4},{8,9},{9,10},{10,1... | collective-permute-start | bytes 3145736 | tf_op jit(solution)/shard_map/ppermute | solution.py:17
  206.6 14.2 %collective-permute-start.1 = (bf16[512,1024]{0,1:T(8,128)(2,1)S(1)}, bf16[512,1024]{0,1:T(8,128)(2,1)S(1)}, u32[]{:S(2)}, u32[]{:S(2)}) collective-permute-start(bf16[512,1024]{0,1:T(8,128)(2,1)S(1)} %collective-permute-done), channel_id=1, source_target_pairs={{0,1},{1,2},{2,3},{3,0},{4,5},{5,6},{6,7},{7,4},{8,9},{9,10},{10,1... | collective-permute-start | bytes 3145736 | tf_op jit(solution)/shard_map/ppermute | solution.py:17
  220.8 14.5 %collective-permute-start.2 = (bf16[512,1024]{0,1:T(8,128)(2,1)S(1)}, bf16[512,1024]{0,1:T(8,128)(2,1)}, u32[]{:S(2)}, u32[]{:S(2)}) collective-permute-start(bf16[512,1024]{0,1:T(8,128)(2,1)S(1)} %collective-permute-done.1), channel_id=1, source_target_pairs={{0,1},{1,2},{2,3},{3,0},{4,5},{5,6},{6,7},{7,4},{8,9},{9,10},{10,1... | collective-permute-start | bytes 3145736 | tf_op jit(solution)/shard_map/ppermute | solution.py:17
  340.3 133.8 %copy-start.2 = (bf16[512,1024]{1,0:T(8,128)(2,1)S(1)}, bf16[512,1024]{1,0:T(8,128)(2,1)}, u32[]{:S(2)}) copy-start(bf16[512,1024]{1,0:T(8,128)(2,1)} %fusion.45) | copy-start | bytes 3145732
  340.3 257.0 %all-gather.18.cloned.1.call-start = ((), (), s32[]{:S(2)}) async-start(), calls=%async_computation.4 | async-start | bytes 9437184 | tf_op jit(solution)/shard_map/all_gather | solution.py:54
  474.0 259.1 %all-gather.20.cloned.1.call-start = ((), (), s32[]{:S(2)}) async-start(), calls=%async_computation.5 | async-start | bytes 9437184 | tf_op jit(solution)/shard_map/all_gather | solution.py:44
  474.1 14.3 %collective-permute-start.3 = (bf16[512,1024]{1,0:T(8,128)(2,1)S(1)}, bf16[512,1024]{1,0:T(8,128)(2,1)S(1)}, u32[]{:S(2)}, u32[]{:S(2)}) collective-permute-start(bf16[512,1024]{1,0:T(8,128)(2,1)S(1)} %copy-done.2), channel_id=1, source_target_pairs={{0,1},{1,2},{2,3},{3,0},{4,5},{5,6},{6,7},{7,4},{8,9},{9,10},{10,1... | collective-permute-start | bytes 3145736 | tf_op jit(solution)/shard_map/ppermute | solution.py:17
  488.4 14.2 %collective-permute-start.4 = (bf16[512,1024]{1,0:T(8,128)(2,1)S(1)}, bf16[512,1024]{1,0:T(8,128)(2,1)S(1)}, u32[]{:S(2)}, u32[]{:S(2)}) collective-permute-start(bf16[512,1024]{1,0:T(8,128)(2,1)S(1)} %collective-permute-done.3), channel_id=1, source_target_pairs={{0,1},{1,2},{2,3},{3,0},{4,5},{5,6},{6,7},{7,4},{8,9},{9,10},{10,1... | collective-permute-start | bytes 3145736 | tf_op jit(solution)/shard_map/ppermute | solution.py:17
  502.6 14.5 %collective-permute-start.5 = (bf16[512,1024]{1,0:T(8,128)(2,1)S(1)}, bf16[512,1024]{1,0:T(8,128)(2,1)}, u32[]{:S(2)}, u32[]{:S(2)}) collective-permute-start(bf16[512,1024]{1,0:T(8,128)(2,1)S(1)} %collective-permute-done.4), channel_id=1, source_target_pairs={{0,1},{1,2},{2,3},{3,0},{4,5},{5,6},{6,7},{7,4},{8,9},{9,10},{10,1... | collective-permute-start | bytes 3145736 | tf_op jit(solution)/shard_map/ppermute | solution.py:17
  610.3 133.8 %copy-start.3 = (bf16[512,1024]{1,0:T(8,128)(2,1)S(1)}, bf16[512,1024]{1,0:T(8,128)(2,1)}, u32[]{:S(2)}) copy-start(bf16[512,1024]{1,0:T(8,128)(2,1)} %fusion.48) | copy-start | bytes 3145732
  610.3 257.0 %all-gather.22.cloned.1.call-start = ((), (), s32[]{:S(2)}) async-start(), calls=%async_computation.6 | async-start | bytes 9437184 | tf_op jit(solution)/shard_map/all_gather | solution.py:54
  744.0 259.1 %all-gather.24.cloned.1.call-start = ((), (), s32[]{:S(2)}) async-start(), calls=%async_computation.7 | async-start | bytes 9437184 | tf_op jit(solution)/shard_map/all_gather | solution.py:44
  744.1 14.3 %collective-permute-start.6 = (bf16[512,1024]{1,0:T(8,128)(2,1)S(1)}, bf16[512,1024]{1,0:T(8,128)(2,1)S(1)}, u32[]{:S(2)}, u32[]{:S(2)}) collective-permute-start(bf16[512,1024]{1,0:T(8,128)(2,1)S(1)} %copy-done.3), channel_id=1, source_target_pairs={{0,1},{1,2},{2,3},{3,0},{4,5},{5,6},{6,7},{7,4},{8,9},{9,10},{10,1... | collective-permute-start | bytes 3145736 | tf_op jit(solution)/shard_map/ppermute | solution.py:17
  758.4 14.2 %collective-permute-start.7 = (bf16[512,1024]{1,0:T(8,128)(2,1)S(1)}, bf16[512,1024]{1,0:T(8,128)(2,1)S(1)}, u32[]{:S(2)}, u32[]{:S(2)}) collective-permute-start(bf16[512,1024]{1,0:T(8,128)(2,1)S(1)} %collective-permute-done.6), channel_id=1, source_target_pairs={{0,1},{1,2},{2,3},{3,0},{4,5},{5,6},{6,7},{7,4},{8,9},{9,10},{10,1... | collective-permute-start | bytes 3145736 | tf_op jit(solution)/shard_map/ppermute | solution.py:17
  772.6 14.6 %collective-permute-start.8 = (bf16[512,1024]{1,0:T(8,128)(2,1)S(1)}, bf16[512,1024]{1,0:T(8,128)(2,1)}, u32[]{:S(2)}, u32[]{:S(2)}) collective-permute-start(bf16[512,1024]{1,0:T(8,128)(2,1)S(1)} %collective-permute-done.7), channel_id=1, source_target_pairs={{0,1},{1,2},{2,3},{3,0},{4,5},{5,6},{6,7},{7,4},{8,9},{9,10},{10,1... | collective-permute-start | bytes 3145736 | tf_op jit(solution)/shard_map/ppermute | solution.py:17
  880.3 260.2 %all-gather.26.cloned.1.call-start = ((), (), s32[]{:S(2)}) async-start(), calls=%async_computation.8 | async-start | bytes 9437184 | tf_op jit(solution)/shard_map/all_gather | solution.py:54
  1003.1 13.4 %copy-start.1 = (bf16[512,1024]{1,0:T(8,128)(2,1)S(1)}, bf16[512,1024]{1,0:T(8,128)(2,1)}, u32[]{:S(2)}) copy-start(bf16[512,1024]{1,0:T(8,128)(2,1)} %fusion.51) | copy-start | bytes 3145732
  1016.5 14.3 %collective-permute-start.9 = (bf16[512,1024]{1,0:T(8,128)(2,1)S(1)}, bf16[512,1024]{1,0:T(8,128)(2,1)S(1)}, u32[]{:S(2)}, u32[]{:S(2)}) collective-permute-start(bf16[512,1024]{1,0:T(8,128)(2,1)S(1)} %copy-done.1), channel_id=1, source_target_pairs={{0,1},{1,2},{2,3},{3,0},{4,5},{5,6},{6,7},{7,4},{8,9},{9,10},{10,1... | collective-permute-start | bytes 3145736 | tf_op jit(solution)/shard_map/ppermute | solution.py:17
  1030.8 14.2 %collective-permute-start.10 = (bf16[512,1024]{1,0:T(8,128)(2,1)S(1)}, bf16[512,1024]{1,0:T(8,128)(2,1)S(1)}, u32[]{:S(2)}, u32[]{:S(2)}) collective-permute-start(bf16[512,1024]{1,0:T(8,128)(2,1)S(1)} %collective-permute-done.9), channel_id=1, source_target_pairs={{0,1},{1,2},{2,3},{3,0},{4,5},{5,6},{6,7},{7,4},{8,9},{9,10},{10,1... | collective-permute-start | bytes 3145736 | tf_op jit(solution)/shard_map/ppermute | solution.py:17
  1045.0 59.6 %collective-permute-start.11 = (bf16[512,1024]{1,0:T(8,128)(2,1)S(1)}, bf16[512,1024]{1,0:T(8,128)(2,1)}, u32[]{:S(2)}, u32[]{:S(2)}) collective-permute-start(bf16[512,1024]{1,0:T(8,128)(2,1)S(1)} %collective-permute-done.10), channel_id=1, source_target_pairs={{0,1},{1,2},{2,3},{3,0},{4,5},{5,6},{6,7},{7,4},{8,9},{9,10},{10,1... | collective-permute-start | bytes 3145736 | tf_op jit(solution)/shard_map/ppermute | solution.py:17
Sparse Core Ops, SparseCore 0:
  11.6 37.4 all-gather.11
  56.2 125.2 all-gather.9
  192.4 123.1 all-gather.13
  340.4 122.6 all-gather.15
  474.2 123.1 all-gather.17
  610.4 122.6 all-gather.19
  744.2 123.1 all-gather.21
  880.4 122.6 all-gather.23
  1016.6 123.8 all-gather.25
